TPU v7x, 32 devices: a whole 2x2x4 slice. The times are simulated.
32 devices in a mesh: dom: 8 (over y, x, core), col: 4 (over z).
Axes of the slice: x: 2, y: 2, z: 4, core: 2. Of those that a mesh axis runs over, the one named last changes fastest.
Arguments:
- features: bfloat16 [65536, 1024], P('dom', 'col')
- weight: bfloat16 [1024, 1024], P(None, 'col'), may hold values from -0.1875 to 0.1875
- out_bias: bfloat16 [1024], P('col'), may hold values from -3 to 3
- local_index: int32 [8, 64, 4], P('dom'), may hold values from 0 to 63
- local_count: int32 [8, 64], P('dom'), may hold values from 1 to 4, as said below
- local_vals: bfloat16 [8, 64, 4, 128, 128], P('dom'), may hold values from -0.1875 to 0.1875
- halo_index: int32 [8, 64, 4], P('dom'), may hold values from 0 to 31
- halo_count: int32 [8, 64], P('dom'), may hold values from 0 to 4, as said below
- halo_vals: bfloat16 [8, 64, 4, 128, 128], P('dom'), may hold values from -0.1875 to 0.1875
- send_rows: int32 [8, 8, 512], P('dom'), may hold values from 0 to 8191
- send_count: int32 [8, 8], P('dom'), may hold values from 0 to 512, as said below
Outputs:
- normalized: bfloat16 [65536, 1024], P('dom', 'col')
- channel_stats: float32 [2, 1024], P(None, 'col')
Inputs may be any that keep to these rules, and one draw needn't show every extreme that they name: `local_index`: slots k >= local_count of a row tile are not used. `local_count`: every partition has a row tile with all 4 slots used. `halo_index`: slots k >= halo_count of a row tile are not used. `halo_count`: every partition has a row tile with all 4 slots used. `send_rows`: slots s >= send_count[q, p] are not used. send_count[p, p] is 0; every partition fills all 512 slots to some other partition.
All inputs are finite; a program needn't handle non-finite values.
Results may differ from a plain program's by a relative error of at most 0.0075.
Values may be sent and summed in bfloat16 or wider, within the bound.
A program may use at most 192 MiB of HBM per device.

v0:
```python
import jax
import jax.numpy as jnp
from jax import lax
from jax.sharding import PartitionSpec as P

TILE = 128
epsilon = 1e-06


def tile_sum(sources, tile_index, tile_count, tile_vals):
    gathered = sources[tile_index]
    keep_mask = jnp.arange(tile_vals.shape[1])[None, :] < tile_count[:, None]
    masked = jnp.where(keep_mask[:, :, None, None], tile_vals, jnp.zeros_like(tile_vals))
    return jnp.einsum("tkij,tkjc->tic", masked, gathered, preferred_element_type=jnp.float32)


def on_device(
    features,
    weight,
    out_bias,
    local_index,
    local_count,
    local_vals,
    halo_index,
    halo_count,
    halo_vals,
    send_rows,
    send_count,
):
    row_count, col_width = features.shape
    peer_count = lax.axis_size("dom")
    slot_total = send_rows.shape[2]
    chosen = features[send_rows[0]]
    keep_mask = jnp.arange(slot_total)[None, :] < send_count[0][:, None]
    outgoing = jnp.where(keep_mask[:, :, None], chosen, jnp.zeros_like(chosen))
    arrived = lax.all_to_all(outgoing, "dom", split_axis=0, concat_axis=0, tiled=True)
    halo_tiles = arrived.reshape(peer_count * slot_total // TILE, TILE, col_width)
    own_tiles = features.reshape(row_count // TILE, TILE, col_width)
    summed = tile_sum(own_tiles, local_index[0], local_count[0], local_vals[0])
    summed = summed + tile_sum(halo_tiles, halo_index[0], halo_count[0], halo_vals[0])
    spread = summed.reshape(row_count, col_width).astype(jnp.bfloat16)
    node_total = row_count * peer_count
    regrouped = lax.all_to_all(spread, "col", split_axis=0, concat_axis=1, tiled=True)
    full_weight, full_bias = (
        lax.all_gather(weight, "col", axis=1, tiled=True),
        lax.all_gather(out_bias.reshape(1, col_width), "col", axis=1, tiled=True),
    )
    mixed_rows = jnp.dot(regrouped, full_weight, preferred_element_type=jnp.float32) + full_bias[
        0
    ].astype(jnp.float32)
    active = jnp.maximum(mixed_rows, 0.0)
    row_power = jnp.mean(active * active, axis=1, keepdims=True)
    scaled = active * lax.rsqrt(row_power + epsilon)
    sum_whole, square_whole = lax.psum(
        (jnp.sum(scaled, axis=0), jnp.sum(scaled * scaled, axis=0)), ("dom", "col")
    )
    normalized = lax.all_to_all(
        scaled.astype(jnp.bfloat16), "col", split_axis=1, concat_axis=0, tiled=True
    )
    column_start = lax.axis_index("col") * col_width
    sum_total = lax.dynamic_slice_in_dim(sum_whole, column_start, col_width, 0)
    square_total = lax.dynamic_slice_in_dim(square_whole, column_start, col_width, 0)
    channel_mean = sum_total / node_total
    channel_var = square_total / node_total - channel_mean * channel_mean
    return (normalized, jnp.stack([channel_mean, channel_var]))


def solution(mesh):
    in_specs = (
        P("dom", "col"),
        P(None, "col"),
        P("col"),
        P("dom", None, None),
        P("dom", None),
        P("dom", None, None, None, None),
        P("dom", None, None),
        P("dom", None),
        P("dom", None, None, None, None),
        P("dom", None, None),
        P("dom", None),
    )
    out_specs = (P("dom", "col"), P(None, "col"))
    return jax.shard_map(
        on_device, mesh=mesh, in_specs=in_specs, out_specs=out_specs, check_vma=False
    )
```

profile of v0, /device:TPU:0, one launch (start us, length us, event | category | flops | bytes accessed | tf_op | source)
XLA Modules:
  0.0 374.6 jit_solution(2426596609186330712)
XLA Ops:
  7.2 0.7 fusion.10
  7.9 0.7 iota_compare_fusion.2
  8.6 15.7 %gather_fusion.1 = bf16[4096,256]{1,0:T(8,128)(2,1)S(1)} fusion(bf16[8192,256]{1,0:T(8,128)(2,1)} %param.11, s32[4096]{0:T(1024)S(1)} %broadcast_clamp_fusion), kind=kCustom, calls=%fused_computation.1 | custom fusion | bytes 4210688 | tf_op jit(solution)/shard_map/gather | solution.py:33
  24.4 0.0 copy-start
  24.4 0.0 copy-start.1
  24.4 1.7 broadcast_select_fusion
  26.1 5.2 %all-to-all-start = ((bf16[8,512,256]{2,1,0:T(8,128)(2,1)}), bf16[8,512,256]{2,1,0:T(8,128)(2,1)S(1)}, u32[]{:S(2)}, u32[]{:S(2)}) async-start(bf16[8,512,256]{2,1,0:T(8,128)(2,1)} %broadcast_select_fusion), calls=%async_computation | async-start | bytes 4194304 | tf_op jit(solution)/shard_map/all_to_all | solution.py:36
  31.3 0.0 copy-done
  31.3 0.1 copy.19
  31.4 0.1 reshape.208
  31.5 0.0 copy-done.1
  31.5 0.1 copy.18
  31.6 0.1 reshape.192
  31.7 0.0 copy-start.2
  31.7 0.0 copy-start.3
  31.7 12.0 %gather_fusion = bf16[256,128,256]{2,1,0:T(8,128)(2,1)} fusion(bf16[64,128,256]{2,1,0:T(8,128)(2,1)} %bitcast.52, s32[1024]{0:T(1024)S(1)} %pad_clamp_fusion.1), kind=kCustom, calls=%fused_computation | custom fusion | bytes 33555456 | tf_op jit(solution)/shard_map/gather | solution.py:11
  43.7 0.0 copy-done.2
  43.7 0.1 iota_compare_fusion
  43.8 0.0 copy-done.3
  43.8 0.1 iota_compare_fusion.1
  43.9 14.0 %all-to-all-done = bf16[8,512,256]{2,1,0:T(8,128)(2,1)S(1)} async-done(((bf16[8,512,256]{2,1,0:T(8,128)(2,1)}), bf16[8,512,256]{2,1,0:T(8,128)(2,1)S(1)}, u32[]{:S(2)}, u32[]{:S(2)}) %all-to-all-start) | async-done | bytes 2097184 | tf_op jit(solution)/shard_map/all_to_all | solution.py:36
  57.9 9.7 %gather_fusion.2 = bf16[256,128,256]{2,1,0:T(8,128)(2,1)} fusion(bf16[32,128,256]{2,1,0:T(8,128)(2,1)S(1)} %bitcast.53, s32[1024]{0:T(1024)S(1)} %pad_clamp_fusion), kind=kCustom, calls=%fused_computation.2 | custom fusion | bytes 33555456 | tf_op jit(solution)/shard_map/gather | solution.py:11
  67.6 13.8 %fusion.1 = f32[64,128,256,1]{2,1,3,0:T(8,128)} fusion(bf16[64,4,128,256]{3,2,1,0:T(8,128)(2,1)} %bitcast.54, bf16[1,64,4,128,128]{4,3,2,1,0:T(8,128)(2,1)} %param.19, pred[64,4]{1,0:T(8,128)(4,1)S(1)} %iota_compare_fusion), kind=kOutput, calls=%fused_computation.6 | convolution fusion | flops 2151677952 | bytes 33554688 | tf_op jit(solution)/shard_map/tkij,tkjc->tic/dot_general | solution.py:14
  81.4 14.0 %fusion = bf16[64,128,256]{2,1,0:T(8,128)(2,1)} fusion(f32[64,128,256,1]{2,1,3,0:T(8,128)} %fusion.1, bf16[64,4,128,256]{3,2,1,0:T(8,128)(2,1)} %bitcast.55, bf16[1,64,4,128,128]{4,3,2,1,0:T(8,128)(2,1)} %param.16, pred[64,4]{1,0:T(8,128)(4,1)S(1)} %iota_compare_fusion.1), kind=kOutput, calls=%fused_computation.4 | convolution fusion | flops 2155872256 | bytes 37748992 | tf_op jit(solution)/shard_map/tkij,tkjc->tic/dot_general | solution.py:14
  95.4 0.0 copy-start.4
  95.4 6.3 %copy.20 = bf16[4,2048,256]{1,2,0:T(8,128)(2,1)} copy(bf16[4,2048,256]{2,1,0:T(8,128)(2,1)} %bitcast.56) | data formatting | bytes 8388608 | tf_op jit(solution)/shard_map/convert_element_type | solution.py:41
  101.6 4.9 %all-to-all-start.1 = ((bf16[4,2048,256]{1,2,0:T(8,128)(2,1)}), bf16[4,2048,256]{1,2,0:T(8,128)(2,1)}, u32[]{:S(2)}, u32[]{:S(2)}) async-start(bf16[4,2048,256]{1,2,0:T(8,128)(2,1)} %copy.20), calls=%async_computation.1 | async-start | bytes 8388608 | tf_op jit(solution)/shard_map/all_to_all | solution.py:43
  106.5 0.0 all-gather.4.cloned.1.call-start
  106.5 0.7 all-gather.4.cloned.1.call-update
  107.2 0.0 copy-done.4
  107.3 103.9 %all-gather.1 = bf16[4,1,256]{2,1,0:T(2,128)(2,1)S(1)} all-gather(bf16[1,1,256]{2,1,0:T(2,128)(2,1)S(1)} %reshape.220), channel_id=2, replica_groups=mesh['dom'=8,'col'=4] {'col'}, dimensions={0}, use_global_device_ids=true | all-gather | bytes 2560 | tf_op jit(solution)/shard_map/all_gather | solution.py:46
  211.2 0.0 all-gather.4.cloned.1.call-done
  211.2 19.8 %all-to-all-done.1 = bf16[4,2048,256]{1,2,0:T(8,128)(2,1)} async-done(((bf16[4,2048,256]{1,2,0:T(8,128)(2,1)}), bf16[4,2048,256]{1,2,0:T(8,128)(2,1)}, u32[]{:S(2)}, u32[]{:S(2)}) %all-to-all-start.1) | async-done | bytes 4194336 | tf_op jit(solution)/shard_map/all_to_all | solution.py:43
  231.0 7.8 %multiply_reduce_fusion.1 = (f32[2048]{0:T(1024)S(1)}, f32[2048,1024]{0,1:T(8,128)S(1)}) fusion(f32[1024]{0:T(1024)S(1)} %bitcast.61, bf16[2048,1024]{0,1:T(8,128)(2,1)} %bitcast.19, bf16[1024,1024]{1,0:T(8,128)(2,1)} %all-gather.4.cloned.1.call-done), kind=kOutput, calls=%fused_computation.10 | convolution fusion | flops 4303353856 | bytes 14692352 | tf_op jit(solution)/shard_map/dot_general | solution.py:48
  238.8 3.5 fusion.6
  242.2 4.8 %all-to-all-start.2 = ((bf16[2048,4,256]{0,2,1:T(8,128)(2,1)}), bf16[2048,4,256]{0,2,1:T(8,128)(2,1)}, u32[]{:S(2)}, u32[]{:S(2)}) async-start(bf16[2048,4,256]{0,2,1:T(8,128)(2,1)} %bitcast.57), calls=%async_computation.2 | async-start | bytes 8388608 | tf_op jit(solution)/shard_map/all_to_all | solution.py:57
  247.1 113.8 %all-reduce = (f32[1024]{0:T(1024)S(1)}, f32[1024]{0:T(1024)S(1)}) all-reduce(f32[1024]{0:T(1024)S(1)} %get-tuple-element.3, f32[1024]{0:T(1024)S(1)} %get-tuple-element.2), channel_id=1, replica_groups=mesh['dom'=8,'col'=4] {'dom','col'}, use_global_device_ids=true, to_apply=%region_4.5 | all-reduce | flops 2048 | bytes 16384 | tf_op jit(solution)/shard_map/psum | solution.py:54
  360.9 0.1 dynamic-slice_multiply_fusion
  361.0 0.6 pad_maximum_fusion
  361.5 0.0 all-to-all-done.2
  361.6 6.2 %copy.21 = bf16[4,2048,256]{2,1,0:T(8,128)(2,1)} copy(bf16[4,2048,256]{1,2,0:T(8,128)(2,1)} %bitcast.22) | data formatting | bytes 8388608 | tf_op jit(solution)/shard_map/all_to_all | solution.py:57
  (9 shorter events, 0.1 us)
Async XLA Ops:
  24.4 6.9 %copy-start = (s32[1,64,4]{1,2,0:T(4,128)S(1)}, s32[1,64,4]{1,2,0:T(4,128)}, u32[]{:S(2)}) copy-start(s32[1,64,4]{1,2,0:T(4,128)} %param.17) | copy-start | bytes 3076
  24.4 7.1 %copy-start.1 = (s32[1,64,4]{1,2,0:T(4,128)S(1)}, s32[1,64,4]{1,2,0:T(4,128)}, u32[]{:S(2)}) copy-start(s32[1,64,4]{1,2,0:T(4,128)} %param.14) | copy-start | bytes 3076
  26.1 31.8 %all-to-all-start = ((bf16[8,512,256]{2,1,0:T(8,128)(2,1)}), bf16[8,512,256]{2,1,0:T(8,128)(2,1)S(1)}, u32[]{:S(2)}, u32[]{:S(2)}) async-start(bf16[8,512,256]{2,1,0:T(8,128)(2,1)} %broadcast_select_fusion), calls=%async_computation | async-start | bytes 4194304 | tf_op jit(solution)/shard_map/all_to_all | solution.py:36
  31.7 12.0 %copy-start.2 = (s32[1,64]{1,0:T(1,128)S(1)}, s32[1,64]{1,0:T(1,128)}, u32[]{:S(2)}) copy-start(s32[1,64]{1,0:T(1,128)} %param.18) | copy-start | bytes 772
  31.7 12.1 %copy-start.3 = (s32[1,64]{1,0:T(1,128)S(1)}, s32[1,64]{1,0:T(1,128)}, u32[]{:S(2)}) copy-start(s32[1,64]{1,0:T(1,128)} %param.15) | copy-start | bytes 772
  95.4 11.9 %copy-start.4 = (bf16[256]{0:T(256)(128)(2,1)S(1)}, bf16[256]{0:T(256)(128)(2,1)}, u32[]{:S(2)}) copy-start(bf16[256]{0:T(256)(128)(2,1)} %param.13) | copy-start | bytes 1540
  101.6 129.3 %all-to-all-start.1 = ((bf16[4,2048,256]{1,2,0:T(8,128)(2,1)}), bf16[4,2048,256]{1,2,0:T(8,128)(2,1)}, u32[]{:S(2)}, u32[]{:S(2)}) async-start(bf16[4,2048,256]{1,2,0:T(8,128)(2,1)} %copy.20), calls=%async_computation.1 | async-start | bytes 8388608 | tf_op jit(solution)/shard_map/all_to_all | solution.py:43
  106.5 104.7 %all-gather.4.cloned.1.call-start = ((), (), s32[]{:S(2)}) async-start(), calls=%async_computation.3 | async-start | bytes 2621440 | tf_op jit(solution)/shard_map/all_gather | solution.py:45
  242.2 119.3 %all-to-all-start.2 = ((bf16[2048,4,256]{0,2,1:T(8,128)(2,1)}), bf16[2048,4,256]{0,2,1:T(8,128)(2,1)}, u32[]{:S(2)}, u32[]{:S(2)}) async-start(bf16[2048,4,256]{0,2,1:T(8,128)(2,1)} %bitcast.57), calls=%async_computation.2 | async-start | bytes 8388608 | tf_op jit(solution)/shard_map/all_to_all | solution.py:57
Sparse Core Ops, SparseCore 0:
  108.9 94.7 all-gather.3
where the time goes:
time: 375 us
  blocking collectives  218 us (58%)
  local copies, waits for them, and re-layouts  50.3 us (13%)
  matrix products  35.5 us (9%)
  waiting for transfers between devices  34.5 us (9%)
  starting transfers between devices  14.9 us (4%)
  between operations  14.2 us (4%)
  other arithmetic  7.48 us (2%)
    psum x1, blocking collectives, on_device(): lax.psum((jnp.sum(scaled, axis=0), jnp.sum(scaled * scaled, axis=0)), ('d...  114 us
    all_gather x1, blocking collectives, on_device(): lax.all_gather(out_bias.reshape(1, col_width), 'col', axis=1, tiled=True)  104 us
    dot_general x2, matrix products, tile_sum(): jnp.einsum('tkij,tkjc->tic', masked, gathered, preferred_element_type=jnp...  27.7 us
    gather x2, local copies, waits for them, and re-layouts, tile_sum(): gathered = sources[tile_index]  21.7 us
    all_to_all x1, waiting for transfers between devices, on_device(): lax.all_to_all(spread, 'col', split_axis=0, concat_axis=1, tiled=True)  19.8 us
    gather x1, local copies, waits for them, and re-layouts, on_device(): chosen = features[send_rows[0]]  15.7 us
    all_to_all x1, waiting for transfers between devices, on_device(): lax.all_to_all(outgoing, 'dom', split_axis=0, concat_axis=0, tiled=True)  14 us
    dot_general x1, matrix products, on_device(): jnp.dot(regrouped, full_weight, preferred_element_type=jnp.float32)  7.76 us
  transfers between devices with their start and end apart: 4, of which 2 were waited for; matrix products, arithmetic and copies ran while one was open for 4% of the time, Pallas kernels for 0%

commit v1 on v0

--- a/solution.py
+++ b/solution.py
@@ -40,7 +40,10 @@
     summed = summed + tile_sum(halo_tiles, halo_index[0], halo_count[0], halo_vals[0])
     spread = summed.reshape(row_count, col_width).astype(jnp.bfloat16)
     node_total = row_count * peer_count
-    regrouped = lax.all_to_all(spread, "col", split_axis=0, concat_axis=1, tiled=True)
+    regrouped = jnp.concatenate(
+        lax.all_to_all(jnp.stack(jnp.split(spread, lax.axis_size("col"), axis=0)), "col", 0, 0),
+        axis=1,
+    )
     full_weight, full_bias = (
         lax.all_gather(weight, "col", axis=1, tiled=True),
         lax.all_gather(out_bias.reshape(1, col_width), "col", axis=1, tiled=True),

time: 375 us -> 378 us (level)
    convert_element_type x1 -> x0, local copies, waits for them, and re-layouts: 6.27 us -> none  [on_device(): spread = summed.reshape(row_count, col_width).astype(jnp.bfloat16)]
    another operation x0 -> x4, local copies, waits for them, and re-layouts: none -> 5.82 us  [on_device(): jnp.stack(jnp.split(spread, lax.axis_size('col'), axis=0))]
  transfers between devices with their start and end apart: 4 -> 4, of which waited for: 2 -> 2; matrix products, arithmetic and copies ran while one was open for 4% -> 3% of each run, Pallas kernels for 0% -> 0%
where the time goes in v1:
time: 378 us; the launch traced here: 377 us
  blocking collectives  218 us (58%)
  local copies, waits for them, and re-layouts  51.5 us (14%)
  waiting for transfers between devices  34.5 us (9%)
  matrix products  33.4 us (9%)
  starting transfers between devices  14.9 us (4%)
  between operations  14.2 us (4%)
  other arithmetic  11 us (3%)
    psum x1, blocking collectives, on_device(): lax.psum((jnp.sum(scaled, axis=0), jnp.sum(scaled * scaled, axis=0)), ('d...  114 us
    all_gather x1, blocking collectives, on_device(): lax.all_gather(out_bias.reshape(1, col_width), 'col', axis=1, tiled=True)  104 us
    dot_general x2, matrix products, tile_sum(): jnp.einsum('tkij,tkjc->tic', masked, gathered, preferred_element_type=jnp...  25.7 us
    gather x2, local copies, waits for them, and re-layouts, tile_sum(): gathered = sources[tile_index]  21.7 us
    all_to_all x1, waiting for transfers between devices, on_device(): lax.all_to_all(jnp.stack(jnp.split(spread, lax.axis_size('col'), axis=0))...  19.8 us
    gather x1, local copies, waits for them, and re-layouts, on_device(): chosen = features[send_rows[0]]  15.7 us
    all_to_all x1, waiting for transfers between devices, on_device(): lax.all_to_all(outgoing, 'dom', split_axis=0, concat_axis=0, tiled=True)  14 us
    dot_general x1, matrix products, on_device(): jnp.dot(regrouped, full_weight, preferred_element_type=jnp.float32)  7.76 us
  transfers between devices with their start and end apart: 4, of which 2 were waited for; matrix products, arithmetic and copies ran while one was open for 3% of the time, Pallas kernels for 0%

profile of v1, /device:TPU:0, one launch (start us, length us, event | category | flops | bytes accessed | tf_op | source)
XLA Modules:
  0.0 377.2 jit_solution(7002946910222332254)
XLA Ops:
  7.2 0.7 fusion.10
  7.9 0.7 iota_compare_fusion.2
  8.6 15.7 %gather_fusion.1 = bf16[4096,256]{1,0:T(8,128)(2,1)S(1)} fusion(bf16[8192,256]{1,0:T(8,128)(2,1)} %param.11, s32[4096]{0:T(1024)S(1)} %broadcast_clamp_fusion), kind=kCustom, calls=%fused_computation.1 | custom fusion | bytes 4210688 | tf_op jit(solution)/shard_map/gather | solution.py:33
  24.4 0.0 copy-start
  24.4 0.0 copy-start.1
  24.4 1.7 broadcast_select_fusion
  26.1 5.2 %all-to-all-start = ((bf16[8,512,256]{2,1,0:T(8,128)(2,1)}), bf16[8,512,256]{2,1,0:T(8,128)(2,1)S(1)}, u32[]{:S(2)}, u32[]{:S(2)}) async-start(bf16[8,512,256]{2,1,0:T(8,128)(2,1)} %broadcast_select_fusion), calls=%async_computation | async-start | bytes 4194304 | tf_op jit(solution)/shard_map/all_to_all | solution.py:36
  31.3 0.0 copy-done
  31.3 0.1 copy.22
  31.4 0.1 reshape.220
  31.5 0.0 copy-done.1
  31.5 0.1 copy.21
  31.6 0.1 reshape.204
  31.7 0.0 copy-start.2
  31.7 0.0 copy-start.3
  31.7 12.0 %gather_fusion = bf16[256,128,256]{2,1,0:T(8,128)(2,1)} fusion(bf16[64,128,256]{2,1,0:T(8,128)(2,1)} %bitcast.55, s32[1024]{0:T(1024)S(1)} %pad_clamp_fusion.1), kind=kCustom, calls=%fused_computation | custom fusion | bytes 33555456 | tf_op jit(solution)/shard_map/gather | solution.py:11
  43.7 0.0 copy-done.2
  43.7 0.1 iota_compare_fusion
  43.8 0.0 copy-done.3
  43.8 0.1 iota_compare_fusion.1
  43.9 14.0 %all-to-all-done = bf16[8,512,256]{2,1,0:T(8,128)(2,1)S(1)} async-done(((bf16[8,512,256]{2,1,0:T(8,128)(2,1)}), bf16[8,512,256]{2,1,0:T(8,128)(2,1)S(1)}, u32[]{:S(2)}, u32[]{:S(2)}) %all-to-all-start) | async-done | bytes 2097184 | tf_op jit(solution)/shard_map/all_to_all | solution.py:36
  57.9 9.7 %gather_fusion.2 = bf16[256,128,256]{2,1,0:T(8,128)(2,1)} fusion(bf16[32,128,256]{2,1,0:T(8,128)(2,1)S(1)} %bitcast.56, s32[1024]{0:T(1024)S(1)} %pad_clamp_fusion), kind=kCustom, calls=%fused_computation.2 | custom fusion | bytes 33555456 | tf_op jit(solution)/shard_map/gather | solution.py:11
  67.6 13.8 %fusion.1 = f32[64,128,256,1]{2,1,3,0:T(8,128)} fusion(bf16[64,4,128,256]{3,2,1,0:T(8,128)(2,1)} %bitcast.57, bf16[1,64,4,128,128]{4,3,2,1,0:T(8,128)(2,1)} %param.19, pred[64,4]{1,0:T(8,128)(4,1)S(1)} %iota_compare_fusion), kind=kOutput, calls=%fused_computation.6 | convolution fusion | flops 2151677952 | bytes 33554688 | tf_op jit(solution)/shard_map/tkij,tkjc->tic/dot_general | solution.py:14
  81.4 11.9 %fusion = bf16[64,128,256]{2,1,0:T(8,128)(2,1)S(1)} fusion(f32[64,128,256,1]{2,1,3,0:T(8,128)} %fusion.1, bf16[64,4,128,256]{3,2,1,0:T(8,128)(2,1)} %bitcast.58, bf16[1,64,4,128,128]{4,3,2,1,0:T(8,128)(2,1)} %param.16, pred[64,4]{1,0:T(8,128)(4,1)S(1)} %iota_compare_fusion.1), kind=kOutput, calls=%fused_computation.4 | convolution fusion | flops 2155872256 | bytes 37748992 | tf_op jit(solution)/shard_map/tkij,tkjc->tic/dot_general | solution.py:14
  93.3 1.6 fusion.13
  94.9 1.5 copy.23
  96.4 2.3 copy.24
  98.7 1.4 copy.25
  100.1 0.6 copy.26
  100.8 0.0 copy-start.4
  100.8 3.5 pad_maximum_fusion
  104.3 4.9 %all-to-all-start.1 = ((bf16[4,2048,256]{1,2,0:T(8,128)(2,1)}), bf16[4,2048,256]{1,2,0:T(8,128)(2,1)}, u32[]{:S(2)}, u32[]{:S(2)}) async-start(bf16[4,2048,256]{1,2,0:T(8,128)(2,1)} %pad_maximum_fusion), calls=%async_computation.1 | async-start | bytes 8388608 | tf_op jit(solution)/shard_map/all_to_all | solution.py:44
  109.1 0.0 all-gather.4.cloned.1.call-start
  109.2 0.7 all-gather.4.cloned.1.call-update
  109.9 0.0 copy-done.4
  109.9 103.9 %all-gather.1 = bf16[4,1,256]{2,1,0:T(2,128)(2,1)S(1)} all-gather(bf16[1,1,256]{2,1,0:T(2,128)(2,1)S(1)} %reshape.232), channel_id=2, replica_groups=mesh['dom'=8,'col'=4] {'col'}, dimensions={0}, use_global_device_ids=true | all-gather | bytes 2560 | tf_op jit(solution)/shard_map/all_gather | solution.py:49
  213.8 0.0 all-gather.4.cloned.1.call-done
  213.8 19.8 %all-to-all-done.1 = bf16[4,2048,256]{1,2,0:T(8,128)(2,1)} async-done(((bf16[4,2048,256]{1,2,0:T(8,128)(2,1)}), bf16[4,2048,256]{1,2,0:T(8,128)(2,1)}, u32[]{:S(2)}, u32[]{:S(2)}) %all-to-all-start.1) | async-done | bytes 4194336 | tf_op jit(solution)/shard_map/all_to_all | solution.py:44
  233.6 7.8 %multiply_reduce_fusion.1 = (f32[2048]{0:T(1024)S(1)}, f32[2048,1024]{0,1:T(8,128)S(1)}) fusion(f32[1024]{0:T(1024)S(1)} %bitcast.67, bf16[2048,1024]{0,1:T(8,128)(2,1)} %bitcast.22, bf16[1024,1024]{1,0:T(8,128)(2,1)} %all-gather.4.cloned.1.call-done), kind=kOutput, calls=%fused_computation.10 | convolution fusion | flops 4303353856 | bytes 14692352 | tf_op jit(solution)/shard_map/dot_general | solution.py:51
  241.4 3.5 fusion.6
  244.9 4.8 %all-to-all-start.2 = ((bf16[2048,4,256]{0,2,1:T(8,128)(2,1)}), bf16[2048,4,256]{0,2,1:T(8,128)(2,1)}, u32[]{:S(2)}, u32[]{:S(2)}) async-start(bf16[2048,4,256]{0,2,1:T(8,128)(2,1)} %bitcast.59), calls=%async_computation.2 | async-start | bytes 8388608 | tf_op jit(solution)/shard_map/all_to_all | solution.py:60
  249.7 113.8 %all-reduce = (f32[1024]{0:T(1024)S(1)}, f32[1024]{0:T(1024)S(1)}) all-reduce(f32[1024]{0:T(1024)S(1)} %get-tuple-element.3, f32[1024]{0:T(1024)S(1)} %get-tuple-element.2), channel_id=1, replica_groups=mesh['dom'=8,'col'=4] {'dom','col'}, use_global_device_ids=true, to_apply=%region_4.5 | all-reduce | flops 2048 | bytes 16384 | tf_op jit(solution)/shard_map/psum | solution.py:57
  363.5 0.1 dynamic-slice_multiply_fusion
  363.6 0.6 pad_maximum_fusion.1
  364.2 0.0 all-to-all-done.2
  364.2 6.2 %copy.27 = bf16[4,2048,256]{2,1,0:T(8,128)(2,1)} copy(bf16[4,2048,256]{1,2,0:T(8,128)(2,1)} %bitcast.25) | data formatting | bytes 8388608 | tf_op jit(solution)/shard_map/all_to_all | solution.py:60
  (9 shorter events, 0.1 us)
Async XLA Ops:
  24.4 6.9 %copy-start = (s32[1,64,4]{1,2,0:T(4,128)S(1)}, s32[1,64,4]{1,2,0:T(4,128)}, u32[]{:S(2)}) copy-start(s32[1,64,4]{1,2,0:T(4,128)} %param.17) | copy-start | bytes 3076
  24.4 7.1 %copy-start.1 = (s32[1,64,4]{1,2,0:T(4,128)S(1)}, s32[1,64,4]{1,2,0:T(4,128)}, u32[]{:S(2)}) copy-start(s32[1,64,4]{1,2,0:T(4,128)} %param.14) | copy-start | bytes 3076
  26.1 31.8 %all-to-all-start = ((bf16[8,512,256]{2,1,0:T(8,128)(2,1)}), bf16[8,512,256]{2,1,0:T(8,128)(2,1)S(1)}, u32[]{:S(2)}, u32[]{:S(2)}) async-start(bf16[8,512,256]{2,1,0:T(8,128)(2,1)} %broadcast_select_fusion), calls=%async_computation | async-start | bytes 4194304 | tf_op jit(solution)/shard_map/all_to_all | solution.py:36
  31.7 12.0 %copy-start.2 = (s32[1,64]{1,0:T(1,128)S(1)}, s32[1,64]{1,0:T(1,128)}, u32[]{:S(2)}) copy-start(s32[1,64]{1,0:T(1,128)} %param.18) | copy-start | bytes 772
  31.7 12.1 %copy-start.3 = (s32[1,64]{1,0:T(1,128)S(1)}, s32[1,64]{1,0:T(1,128)}, u32[]{:S(2)}) copy-start(s32[1,64]{1,0:T(1,128)} %param.15) | copy-start | bytes 772
  100.8 9.1 %copy-start.4 = (bf16[256]{0:T(256)(128)(2,1)S(1)}, bf16[256]{0:T(256)(128)(2,1)}, u32[]{:S(2)}) copy-start(bf16[256]{0:T(256)(128)(2,1)} %param.13) | copy-start | bytes 1540
  104.3 129.3 %all-to-all-start.1 = ((bf16[4,2048,256]{1,2,0:T(8,128)(2,1)}), bf16[4,2048,256]{1,2,0:T(8,128)(2,1)}, u32[]{:S(2)}, u32[]{:S(2)}) async-start(bf16[4,2048,256]{1,2,0:T(8,128)(2,1)} %pad_maximum_fusion), calls=%async_computation.1 | async-start | bytes 8388608 | tf_op jit(solution)/shard_map/all_to_all | solution.py:44
  109.1 104.7 %all-gather.4.cloned.1.call-start = ((), (), s32[]{:S(2)}) async-start(), calls=%async_computation.3 | async-start | bytes 2621440 | tf_op jit(solution)/shard_map/all_gather | solution.py:48
  244.9 119.3 %all-to-all-start.2 = ((bf16[2048,4,256]{0,2,1:T(8,128)(2,1)}), bf16[2048,4,256]{0,2,1:T(8,128)(2,1)}, u32[]{:S(2)}, u32[]{:S(2)}) async-start(bf16[2048,4,256]{0,2,1:T(8,128)(2,1)} %bitcast.59), calls=%async_computation.2 | async-start | bytes 8388608 | tf_op jit(solution)/shard_map/all_to_all | solution.py:60
Sparse Core Ops, SparseCore 0:
  111.5 94.7 all-gather.3
